TPU v7x, 128 devices: a whole 4x4x4 slice. The times are simulated.
128 devices in a mesh: grp: 16 (over z, x), ep: 8 (over y, core).
Axes of the slice: x: 4, y: 4, z: 4, core: 2. Of those that a mesh axis runs over, the one named last changes fastest.
Arguments:
- tokens: bfloat16 [256, 7168], P(('grp', 'ep')), may hold values from -6 to 6
- expert_ids: int32 [256, 8], P(('grp', 'ep')), may hold values from 0 to 15, all different within a row; in each aligned block of 2 rows (0 to 1, 2 to 3, ...) at most 2 rows name the same one
- gate_ints: int32 [256, 8], P(('grp', 'ep')), may hold values from 1 to 16
- w_gate: bfloat16 [16, 7168, 2048], P('grp', None, 'ep'), may hold values from -0.0625 to 0.0625
- w_up: bfloat16 [16, 7168, 2048], P('grp', None, 'ep'), may hold values from -0.0625 to 0.0625
- w_down: bfloat16 [16, 2048, 7168], P('grp', 'ep'), may hold values from -0.125 to 0.125
Outputs:
- mixed: bfloat16 [256, 7168], P(('grp', 'ep'))
Inputs may be any that keep to these rules, and one draw needn't show every extreme that they name: `expert_ids`: each row names 8 different experts. Within the 2 rows of one device no expert is named more than 2 times, a bound that some block reaches on some device in every draw.
All inputs are finite; a program needn't handle non-finite values.
Results may differ from a plain program's by a relative error of at most 0.015.
Values may be sent and summed in bfloat16 or wider, within the bound.
No kernel may reach another device: no remote copies, remote signals or barrier semaphores. Data moves between devices by JAX's collectives and lax.ppermute only.
A program may use at most 64 MiB of HBM per device.

v0:
```python
import jax
import jax.numpy as jnp
from jax import lax
from jax.sharding import PartitionSpec as P


def local(tokens, expert_ids, gate_ints, w_gate, w_up, w_down):
    groups = lax.axis_size("grp")
    tok_rows, width = tokens.shape
    picks = expert_ids.shape[1]
    capacity = min(tok_rows, max(2, 3 * tok_rows * picks // (2 * groups)))
    routes = expert_ids.reshape(-1)
    onehot = (routes[:, None] == jnp.arange(groups, dtype=jnp.int32)[None, :]).astype(jnp.int32)
    earlier = jnp.cumsum(onehot, axis=0) - onehot
    slots = jnp.sum(earlier * onehot, axis=1)
    position = routes * capacity + slots
    token_index = jnp.arange(tok_rows * picks, dtype=jnp.int32) // picks
    table = jnp.zeros((groups * capacity,), jnp.int32).at[position].set(token_index)
    filled = jnp.zeros((groups * capacity,), jnp.bfloat16).at[position].set(1.0)
    dispatch = (tokens[table] * filled[:, None]).reshape(groups, capacity, width)
    gate_w = w_gate[0]
    up_w = w_up[0]
    down_w = w_down[0]
    arrived = lax.all_to_all(dispatch, "grp", split_axis=0, concat_axis=0, tiled=True)
    arrived = arrived.reshape(groups * capacity, width)
    rows = lax.all_gather(arrived, "ep", axis=0, tiled=True)
    gate = jnp.dot(rows, gate_w, preferred_element_type=jnp.float32)
    up = jnp.dot(rows, up_w, preferred_element_type=jnp.float32)
    hidden = (jax.nn.silu(gate) * up).astype(jnp.bfloat16)
    summed = lax.psum_scatter(
        jnp.dot(hidden, down_w, preferred_element_type=jnp.float32).astype(jnp.bfloat16),
        "ep",
        scatter_dimension=0,
        tiled=True,
    ).astype(jnp.float32)
    summed = summed.astype(jnp.bfloat16).reshape(groups, capacity, width)
    expert_out = lax.all_to_all(summed, "grp", split_axis=0, concat_axis=0, tiled=True)
    flat_out = expert_out.reshape(groups * capacity, width)
    picked = flat_out[position].astype(jnp.float32)
    scores = gate_ints.astype(jnp.float32)
    weight = scores / jnp.sum(scores, axis=1, keepdims=True)
    mixed = jnp.sum(picked.reshape(tok_rows, picks, width) * weight[:, :, None], axis=1)
    return mixed.astype(jnp.bfloat16)


def solution(mesh):
    in_specs = (
        P(("grp", "ep"), None),
        P(("grp", "ep"), None),
        P(("grp", "ep"), None),
        P("grp", None, "ep"),
        P("grp", None, "ep"),
        P("grp", "ep", None),
    )
    out_specs = P(("grp", "ep"), None)
    return jax.shard_map(local, mesh=mesh, in_specs=in_specs, out_specs=out_specs, check_vma=False)
```

profile of v0, /device:TPU:0, one launch (start us, length us, event | category | flops | bytes accessed | tf_op | source)
XLA Modules:
  0.0 137.2 jit_solution(14040806807213435363)
XLA Ops:
  6.5 0.8 eq.15
  7.3 0.7 broadcast_multiply_fusion.1
  8.1 0.2 select_reduce_fusion
  8.3 0.1 mul.43
  8.4 0.6 scatter_custom_fusion
  9.0 0.8 gather_fusion
  9.9 0.2 gather.9
  10.1 0.7 scatter_custom_fusion.1
  10.7 0.1 mul.45
  10.8 0.5 broadcast_multiply_fusion
  11.3 18.6 %all_to_all.10 = bf16[16,2,7168]{2,1,0:T(2,128)(2,1)S(1)} all-to-all(bf16[16,2,7168]{2,1,0:T(2,128)(2,1)S(1)} %broadcast_multiply_fusion), channel_id=1, replica_groups=mesh['grp'=16,'ep'=8] {'grp'}, dimensions={0} | all-to-all | bytes 917504 | tf_op jit(solution)/shard_map/all_to_all | solution.py:24
  29.9 0.9 reshape.53
  30.9 27.6 %all-gather.2.cloned.1.call-done = bf16[256,7168]{1,0:T(8,128)(2,1)} async-done(((bf16[32,7168]{1,0:T(8,128)(2,1)}), bf16[256,7168]{1,0:T(8,128)(2,1)}) %all-gather.2.cloned.1.call-update) | async-done | bytes 3670032 | tf_op jit(solution)/shard_map/all_gather | solution.py:26
  58.5 4.3 %fusion.3 = f32[256,256]{1,0:T(8,128)S(1)} fusion(bf16[256,7168]{1,0:T(8,128)(2,1)} %all-gather.2.cloned.1.call-done, bf16[1,7168,256]{2,1,0:T(8,128)(2,1)} %param.9), kind=kOutput, calls=%fused_computation.8 | convolution fusion | flops 939524096 | bytes 7602176 | tf_op jit(solution)/shard_map/dot_general | solution.py:27
  62.8 10.0 %convolution_convert_fusion = bf16[256,7168]{1,0:T(8,128)(2,1)} fusion(bf16[1,256,7168]{2,1,0:T(8,128)(2,1)} %param.11, bf16[256,7168]{1,0:T(8,128)(2,1)} %all-gather.2.cloned.1.call-done, bf16[1,7168,256]{2,1,0:T(8,128)(2,1)} %param.10, f32[256,256]{1,0:T(8,128)S(1)} %fusion.3), kind=kOutput, calls=%fused_computation.4 | convolution fusion | flops 1881276416 | bytes 14942208 | tf_op jit(solution)/shard_map/dot_general | solution.py:31
  72.9 37.0 %reduce-scatter.2.cloned.1.call-done = bf16[32,7168]{1,0:T(8,128)(2,1)} async-done(((bf16[256,7168]{1,0:T(8,128)(2,1)}), bf16[32,7168]{1,0:T(8,128)(2,1)}) %reduce-scatter.2.cloned.1.call-update) | async-done | bytes 458768 | tf_op jit(solution)/shard_map/reduce_scatter | solution.py:30
  109.9 2.0 %reshape.54 = bf16[16,2,7168]{2,1,0:T(2,128)(2,1)} reshape(bf16[32,7168]{1,0:T(8,128)(2,1)} %reduce-scatter.2.cloned.1.call-done) | data formatting | bytes 917504 | tf_op jit(solution)/shard_map/reshape | solution.py:36
  111.9 6.9 %all-to-all-start.1 = ((bf16[16,2,7168]{2,1,0:T(2,128)(2,1)}), bf16[16,2,7168]{2,1,0:T(2,128)(2,1)S(1)}, u32[]{:S(2)}, u32[]{:S(2)}) async-start(bf16[16,2,7168]{2,1,0:T(2,128)(2,1)} %reshape.54), calls=%async_computation.2 | async-start | bytes 917504 | tf_op jit(solution)/shard_map/all_to_all | solution.py:37
  118.8 0.1 convert_reduce_fusion
  119.0 0.1 convert_divide_fusion
  119.0 9.5 %all-to-all-done.1 = bf16[16,2,7168]{2,1,0:T(2,128)(2,1)S(1)} async-done(((bf16[16,2,7168]{2,1,0:T(2,128)(2,1)}), bf16[16,2,7168]{2,1,0:T(2,128)(2,1)S(1)}, u32[]{:S(2)}, u32[]{:S(2)}) %all-to-all-start.1) | async-done | bytes 458784 | tf_op jit(solution)/shard_map/all_to_all | solution.py:37
  128.6 0.2 reshape.55
  128.8 0.7 gather_fusion.1
  129.4 0.9 fusion.13
  (16 shorter events, 0.2 us)
Async XLA Ops:
  6.5 2.5 %copy-start = (bf16[2,7168]{1,0:T(2,128)(2,1)S(1)}, bf16[2,7168]{1,0:T(2,128)(2,1)}, u32[]{:S(2)}) copy-start(bf16[2,7168]{1,0:T(2,128)(2,1)} %param.6) | copy-start | bytes 86020
  6.5 52.0 %all-gather.2.cloned.1.call-start = ((), (), s32[]{:S(2)}) async-start(), calls=%async_computation.3 | async-start | bytes 4128768 | tf_op jit(solution)/shard_map/all_gather | solution.py:26
  30.9 79.1 %reduce-scatter.2.cloned.1.call-start = ((), (), s32[]{:S(2)}) async-start(), calls=%async_computation.4 | async-start | bytes 4128768 | tf_op jit(solution)/shard_map/reduce_scatter | solution.py:30
  72.9 46.0 %copy-start.1 = (s32[2,8]{1,0:T(2,128)S(1)}, s32[2,8]{1,0:T(2,128)}, u32[]{:S(2)}) copy-start(s32[2,8]{1,0:T(2,128)} %param.8) | copy-start | bytes 196
  111.9 16.7 %all-to-all-start.1 = ((bf16[16,2,7168]{2,1,0:T(2,128)(2,1)}), bf16[16,2,7168]{2,1,0:T(2,128)(2,1)S(1)}, u32[]{:S(2)}, u32[]{:S(2)}) async-start(bf16[16,2,7168]{2,1,0:T(2,128)(2,1)} %reshape.54), calls=%async_computation.2 | async-start | bytes 917504 | tf_op jit(solution)/shard_map/all_to_all | solution.py:37
Sparse Core Ops, SparseCore 0:
  31.0 27.5 all-gather.1
  73.0 36.8 reduce-scatter.1
where the time goes:
time: 138 us; the launch traced here: 137 us
  waiting for transfers between devices  74.2 us (54%)
  blocking collectives  18.6 us (13%)
  matrix products  14.3 us (10%)
  between operations  13.5 us (10%)
  local copies, waits for them, and re-layouts  7 us (5%)
  starting transfers between devices  6.99 us (5%)
  other arithmetic  2.53 us (2%)
    reduce_scatter x1, waiting for transfers between devices, local(): lax.psum_scatter(jnp.dot(hidden, down_w, preferred_element_type=jnp.float...  37 us
    all_gather x1, waiting for transfers between devices, local(): rows = lax.all_gather(arrived, 'ep', axis=0, tiled=True)  27.6 us
    all_to_all x1, blocking collectives, local(): lax.all_to_all(dispatch, 'grp', split_axis=0, concat_axis=0, tiled=True)  18.6 us
    dot_general x1, matrix products, local(): jnp.dot(hidden, down_w, preferred_element_type=jnp.float32)  10 us
    all_to_all x1, waiting for transfers between devices, local(): lax.all_to_all(summed, 'grp', split_axis=0, concat_axis=0, tiled=True)  9.54 us
    all_to_all x1, starting transfers between devices, local(): lax.all_to_all(summed, 'grp', split_axis=0, concat_axis=0, tiled=True)  6.95 us
    dot_general x1, matrix products, local(): gate = jnp.dot(rows, gate_w, preferred_element_type=jnp.float32)  4.26 us
  transfers between devices with their start and end apart: 3, of which 3 were waited for; matrix products, arithmetic and copies ran while one was open for 0% of the time, Pallas kernels for 0%

commit v1 on v0

--- a/solution.py
+++ b/solution.py
@@ -2,6 +2,12 @@
 import jax.numpy as jnp
 from jax import lax
 from jax.sharding import PartitionSpec as P
+
+
+def in_order(blocks, dim):
+    shape = list(blocks.shape[1:])
+    shape[dim] *= blocks.shape[0]
+    return jnp.moveaxis(blocks, 0, dim).reshape(shape)
 
 
 def local(tokens, expert_ids, gate_ints, w_gate, w_up, w_down):
@@ -23,7 +29,19 @@
     down_w = w_down[0]
     arrived = lax.all_to_all(dispatch, "grp", split_axis=0, concat_axis=0, tiled=True)
     arrived = arrived.reshape(groups * capacity, width)
-    rows = lax.all_gather(arrived, "ep", axis=0, tiled=True)
+    count = lax.axis_size("ep")
+    pairs = [(i, (i + 1) % count) for i in range(count)]
+    back = [(b, a) for a, b in pairs]
+    lower, upper = ([], [])
+    for lap in range(count - 1):
+        if lap % 2 == 0:
+            lower.append(lax.ppermute(lower[-1] if lower else arrived, "ep", pairs))
+        else:
+            upper.append(lax.ppermute(upper[-1] if upper else arrived, "ep", back))
+    blocks = jnp.stack([*lower[::-1], arrived, *upper])
+    shift = lax.axis_index("ep") - len(lower)
+    blocks = blocks[(jnp.arange(count) - shift) % count]
+    rows = in_order(blocks, 0)
     gate = jnp.dot(rows, gate_w, preferred_element_type=jnp.float32)
     up = jnp.dot(rows, up_w, preferred_element_type=jnp.float32)
     hidden = (jax.nn.silu(gate) * up).astype(jnp.bfloat16)

time: 138 us -> 153 us (1.11)
  local copies, waits for them, and re-layouts: 7 us -> 18.5 us
  starting transfers between devices: 6.99 us -> 15.9 us
  waiting for transfers between devices: 74.2 us -> 69.2 us
    all_gather x1 -> x0, waiting for transfers between devices: 27.6 us -> none  [local(): rows = lax.all_gather(arrived, 'ep', axis=0, tiled=True)]
    ppermute x0 -> x7, waiting for transfers between devices: none -> 27.5 us  [the longest x4 27.4 us: local(): lower.append(lax.ppermute(lower[-1] if lower else arrived, 'ep', pairs))]
    ppermute x0 -> x7, starting transfers between devices: none -> 8.9 us  [the longest x3 8.87 us: local(): upper.append(lax.ppermute(upper[-1] if upper else arrived, 'ep', back))]
    unnamed x4 -> x11, local copies, waits for them, and re-layouts: 0.01 us -> 6.7 us
    reduce_scatter x1, waiting for transfers between devices: 37 us -> 32.1 us  [local(): lax.psum_scatter(jnp.dot(hidden, down_w, preferred_element_type=jnp.float...]
    gather x0 -> x1, local copies, waits for them, and re-layouts: none -> 4.65 us  [local(): blocks = blocks[(jnp.arange(count) - shift) % count]]
  transfers between devices with their start and end apart: 3 -> 9, of which waited for: 3 -> 6; matrix products, arithmetic and copies ran while one was open for 0% -> 5% of each run, Pallas kernels for 0% -> 0%
where the time goes in v1:
time: 153 us; the launch traced here: 152 us
  waiting for transfers between devices  69.2 us (45%)
  blocking collectives  18.6 us (12%)
  local copies, waits for them, and re-layouts  18.5 us (12%)
  starting transfers between devices  15.9 us (10%)
  matrix products  14.3 us (9%)
  between operations  13.5 us (9%)
  other arithmetic  2.55 us (2%)
    reduce_scatter x1, waiting for transfers between devices, local(): lax.psum_scatter(jnp.dot(hidden, down_w, preferred_element_type=jnp.float...  32.1 us
    ppermute x4, waiting for transfers between devices, local(): lower.append(lax.ppermute(lower[-1] if lower else arrived, 'ep', pairs))  27.4 us
    all_to_all x1, blocking collectives, local(): lax.all_to_all(dispatch, 'grp', split_axis=0, concat_axis=0, tiled=True)  18.6 us
    dot_general x1, matrix products, local(): jnp.dot(hidden, down_w, preferred_element_type=jnp.float32)  10 us
    all_to_all x1, waiting for transfers between devices, local(): lax.all_to_all(summed, 'grp', split_axis=0, concat_axis=0, tiled=True)  9.54 us
    ppermute x3, starting transfers between devices, local(): upper.append(lax.ppermute(upper[-1] if upper else arrived, 'ep', back))  8.87 us
    all_to_all x1, starting transfers between devices, local(): lax.all_to_all(summed, 'grp', split_axis=0, concat_axis=0, tiled=True)  6.96 us
    unnamed x11, local copies, waits for them, and re-layouts  6.7 us
  transfers between devices with their start and end apart: 9, of which 6 were waited for; matrix products, arithmetic and copies ran while one was open for 5% of the time, Pallas kernels for 0%

profile of v1, /device:TPU:0, one launch (start us, length us, event | category | flops | bytes accessed | tf_op | source)
XLA Modules:
  0.0 152.5 jit_solution(3803819207867826928)
XLA Ops:
  9.0 0.8 gather_fusion
  11.3 18.6 %all_to_all.10 = bf16[16,2,7168]{2,1,0:T(2,128)(2,1)S(1)} all-to-all(bf16[16,2,7168]{2,1,0:T(2,128)(2,1)S(1)} %broadcast_multiply_fusion), channel_id=1, replica_groups=mesh['grp'=16,'ep'=8] {'grp'}, dimensions={0} | all-to-all | bytes 917504 | tf_op jit(solution)/shard_map/all_to_all | solution.py:30
  30.1 9.1 %collective-permute-done = bf16[32,7168]{1,0:T(8,128)(2,1)S(1)} collective-permute-done((bf16[32,7168]{1,0:T(8,128)(2,1)S(1)}, bf16[32,7168]{1,0:T(8,128)(2,1)S(1)}, u32[]{:S(2)}, u32[]{:S(2)}) %collective-permute-start) | collective-permute-done | bytes 458784 | tf_op jit(solution)/shard_map/ppermute | solution.py:38
  39.2 3.0 %collective-permute-start.4 = (bf16[32,7168]{1,0:T(8,128)(2,1)S(1)}, bf16[32,7168]{1,0:T(8,128)(2,1)S(1)}, u32[]{:S(2)}, u32[]{:S(2)}) collective-permute-start(bf16[32,7168]{1,0:T(8,128)(2,1)S(1)} %reshape.105), channel_id=1, source_target_pairs={{1,0},{2,1},{3,2},{4,3},{5,4},{6,5},{7,6},{0,7},{9,8},{10,9},{11,1... | collective-permute-start | bytes 1376264 | tf_op jit(solution)/shard_map/ppermute | solution.py:40
  42.1 6.2 %collective-permute-done.1 = bf16[32,7168]{1,0:T(8,128)(2,1)S(1)} collective-permute-done((bf16[32,7168]{1,0:T(8,128)(2,1)S(1)}, bf16[32,7168]{1,0:T(8,128)(2,1)S(1)}, u32[]{:S(2)}, u32[]{:S(2)}) %collective-permute-start.1) | collective-permute-done | bytes 458784 | tf_op jit(solution)/shard_map/ppermute | solution.py:38
  48.3 3.0 %collective-permute-start.5 = (bf16[32,7168]{1,0:T(8,128)(2,1)S(1)}, bf16[32,7168]{1,0:T(8,128)(2,1)S(1)}, u32[]{:S(2)}, u32[]{:S(2)}) collective-permute-start(bf16[32,7168]{1,0:T(8,128)(2,1)S(1)} %collective-permute-done.4), channel_id=1, source_target_pairs={{1,0},{2,1},{3,2},{4,3},{5,4},{6,5},{7,6},{0,7},{9,8},{10,9},{11,1... | collective-permute-start | bytes 1376264 | tf_op jit(solution)/shard_map/ppermute | solution.py:40
  51.3 6.2 %collective-permute-done.2 = bf16[32,7168]{1,0:T(8,128)(2,1)S(1)} collective-permute-done((bf16[32,7168]{1,0:T(8,128)(2,1)S(1)}, bf16[32,7168]{1,0:T(8,128)(2,1)S(1)}, u32[]{:S(2)}, u32[]{:S(2)}) %collective-permute-start.2) | collective-permute-done | bytes 458784 | tf_op jit(solution)/shard_map/ppermute | solution.py:38
  57.6 3.0 %collective-permute-start.6 = (bf16[32,7168]{1,0:T(8,128)(2,1)S(1)}, bf16[32,7168]{1,0:T(8,128)(2,1)S(1)}, u32[]{:S(2)}, u32[]{:S(2)}) collective-permute-start(bf16[32,7168]{1,0:T(8,128)(2,1)S(1)} %collective-permute-done.5), channel_id=1, source_target_pairs={{1,0},{2,1},{3,2},{4,3},{5,4},{6,5},{7,6},{0,7},{9,8},{10,9},{11,1... | collective-permute-start | bytes 1376264 | tf_op jit(solution)/shard_map/ppermute | solution.py:40
  60.6 6.0 %collective-permute-done.3 = bf16[32,7168]{1,0:T(8,128)(2,1)} collective-permute-done((bf16[32,7168]{1,0:T(8,128)(2,1)S(1)}, bf16[32,7168]{1,0:T(8,128)(2,1)}, u32[]{:S(2)}, u32[]{:S(2)}) %collective-permute-start.3) | collective-permute-done | bytes 458784 | tf_op jit(solution)/shard_map/ppermute | solution.py:38
  66.6 1.8 %bitcast_dynamic-update-slice_fusion.6 = bf16[8,32,7168]{2,1,0:T(8,128)(2,1)} fusion(bf16[32,7168]{1,0:T(8,128)(2,1)} %collective-permute-done.3), kind=kLoop, calls=%fused_computation.21 | loop fusion | bytes 917504
  68.5 0.8 bitcast_dynamic-update-slice_fusion.5
  69.3 0.8 bitcast_dynamic-update-slice_fusion.4
  70.1 0.8 bitcast_dynamic-update-slice_fusion.3
  70.9 0.8 constant_dynamic-update-slice_fusion
  71.7 0.8 bitcast_dynamic-update-slice_fusion.2
  72.5 0.8 bitcast_dynamic-update-slice_fusion.1
  74.1 4.7 %gather_fusion.1 = bf16[8,32,7168]{2,1,0:T(8,128)(2,1)} fusion(bf16[8,32,7168]{2,1,0:T(8,128)(2,1)} %bitcast_dynamic-update-slice_fusion, s32[1024]{0:T(1024)S(1)} %pad_clamp_fusion.1), kind=kCustom, calls=%fused_computation.1 | custom fusion | bytes 7340064 | tf_op jit(solution)/shard_map/gather | solution.py:43
  78.8 4.3 %fusion.3 = f32[256,256]{1,0:T(8,128)S(1)} fusion(bf16[256,7168]{1,0:T(8,128)(2,1)} %bitcast.43, bf16[1,7168,256]{2,1,0:T(8,128)(2,1)} %param.9), kind=kOutput, calls=%fused_computation.9 | convolution fusion | flops 939524096 | bytes 7602176 | tf_op jit(solution)/shard_map/dot_general | solution.py:45
  83.1 10.0 %convolution_convert_fusion = bf16[256,7168]{1,0:T(8,128)(2,1)} fusion(bf16[1,256,7168]{2,1,0:T(8,128)(2,1)} %param.11, bf16[256,7168]{1,0:T(8,128)(2,1)} %bitcast.44, bf16[1,7168,256]{2,1,0:T(8,128)(2,1)} %param.10, f32[256,256]{1,0:T(8,128)S(1)} %fusion.3), kind=kOutput, calls=%fused_computation.5 | convolution fusion | flops 1881276416 | bytes 14942208 | tf_op jit(solution)/shard_map/dot_general | solution.py:49
  93.1 32.1 %reduce-scatter.2.cloned.1.call-done = bf16[32,7168]{1,0:T(8,128)(2,1)} async-done(((bf16[256,7168]{1,0:T(8,128)(2,1)}), bf16[32,7168]{1,0:T(8,128)(2,1)}) %reduce-scatter.2.cloned.1.call-update) | async-done | bytes 458768 | tf_op jit(solution)/shard_map/reduce_scatter | solution.py:48
  125.2 2.0 %reshape.107 = bf16[16,2,7168]{2,1,0:T(2,128)(2,1)} reshape(bf16[32,7168]{1,0:T(8,128)(2,1)} %reduce-scatter.2.cloned.1.call-done) | data formatting | bytes 917504 | tf_op jit(solution)/shard_map/reshape | solution.py:54
  127.2 7.0 %all-to-all-start.1 = ((bf16[16,2,7168]{2,1,0:T(2,128)(2,1)}), bf16[16,2,7168]{2,1,0:T(2,128)(2,1)S(1)}, u32[]{:S(2)}, u32[]{:S(2)}) async-start(bf16[16,2,7168]{2,1,0:T(2,128)(2,1)} %reshape.107), calls=%async_computation.2 | async-start | bytes 917504 | tf_op jit(solution)/shard_map/all_to_all | solution.py:55
  134.4 9.5 %all-to-all-done.1 = bf16[16,2,7168]{2,1,0:T(2,128)(2,1)S(1)} async-done(((bf16[16,2,7168]{2,1,0:T(2,128)(2,1)}), bf16[16,2,7168]{2,1,0:T(2,128)(2,1)S(1)}, u32[]{:S(2)}, u32[]{:S(2)}) %all-to-all-start.1) | async-done | bytes 458784 | tf_op jit(solution)/shard_map/all_to_all | solution.py:55
  144.8 0.9 fusion.13
  (39 shorter events, 6.2 us)
Async XLA Ops:
  6.5 2.5 %copy-start = (bf16[2,7168]{1,0:T(2,128)(2,1)S(1)}, bf16[2,7168]{1,0:T(2,128)(2,1)}, u32[]{:S(2)}) copy-start(bf16[2,7168]{1,0:T(2,128)(2,1)} %param.6) | copy-start | bytes 86020
  6.5 118.7 %reduce-scatter.2.cloned.1.call-start = ((), (), s32[]{:S(2)}) async-start(), calls=%async_computation.3 | async-start | bytes 4128768 | tf_op jit(solution)/shard_map/reduce_scatter | solution.py:48
  30.1 9.1 %collective-permute-start = (bf16[32,7168]{1,0:T(8,128)(2,1)S(1)}, bf16[32,7168]{1,0:T(8,128)(2,1)S(1)}, u32[]{:S(2)}, u32[]{:S(2)}) collective-permute-start(bf16[32,7168]{1,0:T(8,128)(2,1)S(1)} %reshape.105), channel_id=1, source_target_pairs={{0,1},{1,2},{2,3},{3,4},{4,5},{5,6},{6,7},{7,0},{8,9},{9,10},{10,1... | collective-permute-start | bytes 1376264 | tf_op jit(solution)/shard_map/ppermute | solution.py:38
  39.2 9.1 %collective-permute-start.1 = (bf16[32,7168]{1,0:T(8,128)(2,1)S(1)}, bf16[32,7168]{1,0:T(8,128)(2,1)S(1)}, u32[]{:S(2)}, u32[]{:S(2)}) collective-permute-start(bf16[32,7168]{1,0:T(8,128)(2,1)S(1)} %collective-permute-done), channel_id=1, source_target_pairs={{0,1},{1,2},{2,3},{3,4},{4,5},{5,6},{6,7},{7,0},{8,9},{9,10},{10,1... | collective-permute-start | bytes 1376264 | tf_op jit(solution)/shard_map/ppermute | solution.py:38
  39.2 9.1 %collective-permute-start.4 = (bf16[32,7168]{1,0:T(8,128)(2,1)S(1)}, bf16[32,7168]{1,0:T(8,128)(2,1)S(1)}, u32[]{:S(2)}, u32[]{:S(2)}) collective-permute-start(bf16[32,7168]{1,0:T(8,128)(2,1)S(1)} %reshape.105), channel_id=1, source_target_pairs={{1,0},{2,1},{3,2},{4,3},{5,4},{6,5},{7,6},{0,7},{9,8},{10,9},{11,1... | collective-permute-start | bytes 1376264 | tf_op jit(solution)/shard_map/ppermute | solution.py:40
  48.3 9.1 %collective-permute-start.2 = (bf16[32,7168]{1,0:T(8,128)(2,1)S(1)}, bf16[32,7168]{1,0:T(8,128)(2,1)S(1)}, u32[]{:S(2)}, u32[]{:S(2)}) collective-permute-start(bf16[32,7168]{1,0:T(8,128)(2,1)S(1)} %collective-permute-done.1), channel_id=1, source_target_pairs={{0,1},{1,2},{2,3},{3,4},{4,5},{5,6},{6,7},{7,0},{8,9},{9,10},{10,1... | collective-permute-start | bytes 1376264 | tf_op jit(solution)/shard_map/ppermute | solution.py:38
  48.3 9.3 %collective-permute-start.5 = (bf16[32,7168]{1,0:T(8,128)(2,1)S(1)}, bf16[32,7168]{1,0:T(8,128)(2,1)S(1)}, u32[]{:S(2)}, u32[]{:S(2)}) collective-permute-start(bf16[32,7168]{1,0:T(8,128)(2,1)S(1)} %collective-permute-done.4), channel_id=1, source_target_pairs={{1,0},{2,1},{3,2},{4,3},{5,4},{6,5},{7,6},{0,7},{9,8},{10,9},{11,1... | collective-permute-start | bytes 1376264 | tf_op jit(solution)/shard_map/ppermute | solution.py:40
  57.4 9.2 %collective-permute-start.3 = (bf16[32,7168]{1,0:T(8,128)(2,1)S(1)}, bf16[32,7168]{1,0:T(8,128)(2,1)}, u32[]{:S(2)}, u32[]{:S(2)}) collective-permute-start(bf16[32,7168]{1,0:T(8,128)(2,1)S(1)} %collective-permute-done.2), channel_id=1, source_target_pairs={{0,1},{1,2},{2,3},{3,4},{4,5},{5,6},{6,7},{7,0},{8,9},{9,10},{10,1... | collective-permute-start | bytes 1376264 | tf_op jit(solution)/shard_map/ppermute | solution.py:38
  57.6 15.7 %collective-permute-start.6 = (bf16[32,7168]{1,0:T(8,128)(2,1)S(1)}, bf16[32,7168]{1,0:T(8,128)(2,1)S(1)}, u32[]{:S(2)}, u32[]{:S(2)}) collective-permute-start(bf16[32,7168]{1,0:T(8,128)(2,1)S(1)} %collective-permute-done.5), channel_id=1, source_target_pairs={{1,0},{2,1},{3,2},{4,3},{5,4},{6,5},{7,6},{0,7},{9,8},{10,9},{11,1... | collective-permute-start | bytes 1376264 | tf_op jit(solution)/shard_map/ppermute | solution.py:40
  93.1 41.1 %copy-start.1 = (s32[2,8]{1,0:T(2,128)S(1)}, s32[2,8]{1,0:T(2,128)}, u32[]{:S(2)}) copy-start(s32[2,8]{1,0:T(2,128)} %param.8) | copy-start | bytes 196
  127.2 16.7 %all-to-all-start.1 = ((bf16[16,2,7168]{2,1,0:T(2,128)(2,1)}), bf16[16,2,7168]{2,1,0:T(2,128)(2,1)S(1)}, u32[]{:S(2)}, u32[]{:S(2)}) async-start(bf16[16,2,7168]{2,1,0:T(2,128)(2,1)} %reshape.107), calls=%async_computation.2 | async-start | bytes 917504 | tf_op jit(solution)/shard_map/all_to_all | solution.py:55
Sparse Core Ops, SparseCore 0:
  93.2 31.9 reduce-scatter.1
